TPU v7x, 64 devices: a 2x2x8 block of a 4x4x8 slice. The times are simulated.
64 devices in a mesh: data: 4 (over x, y), model: 16 (over z, core).
Axes of the slice: x: 2, y: 2, z: 8, core: 2. Of those that a mesh axis runs over, the one named last changes fastest.
The devices are a block of a 4x4x8 slice.
Arguments:
- hidden_in: bfloat16 [4, 4096, 1536], P('data', 'model'), parts along dimension 0
- seg_ids: int32 [4, 4096], P('data'), parts along dimension 0
- gain_attn: bfloat16 [1536], replicated
- w_qkv: bfloat16 [1536, 16, 3, 96], P(None, 'model')
- w_out: bfloat16 [16, 96, 1536], P('model')
- gain_mlp: bfloat16 [1536], replicated
- w_up: bfloat16 [1536, 6144], P(None, 'model')
- w_down: bfloat16 [6144, 1536], P('model')
- grad_out: bfloat16 [4, 4096, 1536], P('data', 'model'), parts along dimension 0
Outputs:
- output 1: bfloat16 [4, 4096, 1536], P('data', 'model'), parts along dimension 0
- output 2: bfloat16 [4, 4096, 1536], P('data', 'model'), parts along dimension 0
- output 3: bfloat16 [6144, 16, 3, 96], P('data', 'model'), parts along dimension 0
- output 4: bfloat16 [64, 96, 1536], P(('data', 'model')), parts along dimension 0
- output 5: bfloat16 [6144, 6144], P('data', 'model'), parts along dimension 0
- output 6: bfloat16 [24576, 1536], P(('data', 'model')), parts along dimension 0
- output 7: bfloat16 [6144], P('data'), parts along dimension 0
- output 8: bfloat16 [6144], P('data'), parts along dimension 0
There are 4 independent parts. A program takes and returns all parts, laid end to end along the dimension named above; an argument that names none is the same for every part.
All inputs are finite; a program needn't handle non-finite values.
Results may differ from a plain program's by a relative error of at most 0.02.
Values are sent between devices in bfloat16 or wider.
A program may use at most 768 MiB of HBM per device.

v0:
```python
import jax
import jax.numpy as jnp
from jax import lax
from jax.sharding import PartitionSpec as P

LN_EPS = 1e-5


def layer_norm(x_f32, gain_f32):
    mean_val = jnp.mean(x_f32, axis=-1, keepdims=True)
    centered = x_f32 - mean_val
    variance = jnp.mean(centered * centered, axis=-1, keepdims=True)
    return centered * lax.rsqrt(variance + LN_EPS) * gain_f32


def gelu_tanh(pre_act):
    return jax.nn.gelu(pre_act, approximate=True)


def attention_fwd(qkv_vals, attn_mask, attn_scale):
    q_part = qkv_vals[:, :, :, 0]
    k_part = qkv_vals[:, :, :, 1]
    v_part = qkv_vals[:, :, :, 2]
    scores = jnp.einsum('bqhe,bkhe->bhqk', q_part, k_part, preferred_element_type=jnp.float32) * attn_scale
    attn_prob = jax.nn.softmax(jnp.where(attn_mask[:, None], scores, -1e30), axis=-1)
    prob_lo = attn_prob.astype(jnp.bfloat16)
    attn_out = jnp.einsum('bhqk,bkhe->bqhe', prob_lo, v_part, preferred_element_type=jnp.float32).astype(jnp.bfloat16)
    return attn_out, attn_prob, prob_lo


def attention_bwd(qkv_vals, attn_out, d_out, attn_prob, prob_lo, attn_scale):
    q_part = qkv_vals[:, :, :, 0]
    k_part = qkv_vals[:, :, :, 1]
    v_part = qkv_vals[:, :, :, 2]
    d_prob = jnp.einsum('bqhe,bkhe->bhqk', d_out, v_part, preferred_element_type=jnp.float32)
    row_delta = jnp.einsum('bqhe,bqhe->bhq', d_out, attn_out, preferred_element_type=jnp.float32)
    d_scores = (attn_prob * (d_prob - row_delta[..., None]) * attn_scale).astype(jnp.bfloat16)
    d_q = jnp.einsum('bhqk,bkhe->bqhe', d_scores, k_part, preferred_element_type=jnp.float32).astype(jnp.bfloat16)
    d_k = jnp.einsum('bhqk,bqhe->bkhe', d_scores, q_part, preferred_element_type=jnp.float32).astype(jnp.bfloat16)
    d_v = jnp.einsum('bhqk,bqhe->bkhe', prob_lo, d_out, preferred_element_type=jnp.float32).astype(jnp.bfloat16)
    return jnp.stack([d_q, d_k, d_v], axis=3)


def local_layer(hidden_in, seg_ids, gain_attn, w_qkv, w_out, gain_mlp, w_up, w_down, grad_out):
    attn_scale = w_out.shape[1] ** -0.5
    seq_len = seg_ids.shape[1]
    positions = jnp.arange(seq_len)
    attn_mask = (positions[:, None] >= positions[None, :])[None] & (seg_ids[:, :, None] == seg_ids[:, None, :])
    x_f32 = hidden_in.astype(jnp.float32)
    ln1_out, ln1_vjp = jax.vjp(layer_norm, x_f32, gain_attn.astype(jnp.float32))
    attn_in = lax.all_gather(ln1_out.astype(jnp.bfloat16), 'model', axis=1, tiled=True)
    qkv_vals = jnp.einsum('bsd,dhce->bshce', attn_in, w_qkv, preferred_element_type=jnp.float32).astype(jnp.bfloat16)
    attn_out, attn_prob, prob_lo = attention_fwd(qkv_vals, attn_mask, attn_scale)
    attn_part = jnp.einsum('bshe,hed->bsd', attn_out, w_out, preferred_element_type=jnp.float32).astype(jnp.bfloat16)
    attn_sum = lax.psum_scatter(attn_part, 'model', scatter_dimension=1, tiled=True)
    mid_loc = (x_f32 + attn_sum.astype(jnp.float32)).astype(jnp.bfloat16)
    ln2_out, ln2_vjp = jax.vjp(layer_norm, mid_loc.astype(jnp.float32), gain_mlp.astype(jnp.float32))
    mlp_in = lax.all_gather(ln2_out.astype(jnp.bfloat16), 'model', axis=1, tiled=True)
    pre_act = jnp.einsum('bsd,df->bsf', mlp_in, w_up, preferred_element_type=jnp.float32)
    act_f32, gelu_vjp = jax.vjp(gelu_tanh, pre_act)
    act_lo = act_f32.astype(jnp.bfloat16)
    mlp_part = jnp.einsum('bsf,fd->bsd', act_lo, w_down, preferred_element_type=jnp.float32).astype(jnp.bfloat16)
    mlp_sum = lax.psum_scatter(mlp_part, 'model', scatter_dimension=1, tiled=True)
    hidden_out = (mid_loc.astype(jnp.float32) + mlp_sum.astype(jnp.float32)).astype(jnp.bfloat16)
    grad_full = lax.all_gather(grad_out, 'model', axis=1, tiled=True)
    d_act = jnp.einsum('bsd,fd->bsf', grad_full, w_down, preferred_element_type=jnp.float32)
    d_pre = gelu_vjp(d_act)[0].astype(jnp.bfloat16)
    g_down = jnp.einsum('bsf,bsd->fd', act_lo, grad_full, preferred_element_type=jnp.float32).astype(jnp.bfloat16)
    d_mlp_part = jnp.einsum('bsf,df->bsd', d_pre, w_up, preferred_element_type=jnp.float32).astype(jnp.bfloat16)
    g_up = jnp.einsum('bsd,bsf->df', mlp_in, d_pre, preferred_element_type=jnp.float32).astype(jnp.bfloat16)
    d_mlp_in = lax.psum_scatter(d_mlp_part, 'model', scatter_dimension=1, tiled=True)
    d_mid_ln, d_gain_mlp = ln2_vjp(d_mlp_in.astype(jnp.float32))
    d_mid = (grad_out.astype(jnp.float32) + d_mid_ln).astype(jnp.bfloat16)
    d_mid_full = lax.all_gather(d_mid, 'model', axis=1, tiled=True)
    d_attn_out = jnp.einsum('bsd,hed->bshe', d_mid_full, w_out, preferred_element_type=jnp.float32).astype(jnp.bfloat16)
    g_out = jnp.einsum('bshe,bsd->hed', attn_out, d_mid_full, preferred_element_type=jnp.float32).astype(jnp.bfloat16)
    d_qkv = attention_bwd(qkv_vals, attn_out, d_attn_out, attn_prob, prob_lo, attn_scale)
    g_qkv = jnp.einsum('bsd,bshce->dhce', attn_in, d_qkv, preferred_element_type=jnp.float32).astype(jnp.bfloat16)
    d_attn_part = jnp.einsum('bshce,dhce->bsd', d_qkv, w_qkv, preferred_element_type=jnp.float32).astype(jnp.bfloat16)
    d_attn_in = lax.psum_scatter(d_attn_part, 'model', scatter_dimension=1, tiled=True)
    d_x_ln, d_gain_attn = ln1_vjp(d_attn_in.astype(jnp.float32))
    grad_in = (d_mid.astype(jnp.float32) + d_x_ln).astype(jnp.bfloat16)
    gain_sums = lax.psum(jnp.stack([d_gain_attn, d_gain_mlp]), 'model')
    return (hidden_out, grad_in, g_qkv, g_out, g_up, g_down, gain_sums[0].astype(jnp.bfloat16), gain_sums[1].astype(jnp.bfloat16))


def solution(mesh):
    act_spec = P('data', 'model', None)
    in_specs = (act_spec, P('data', None), P(), P(None, 'model', None, None), P('model', None, None), P(), P(None, 'model'), P('model', None), act_spec)
    out_specs = (act_spec, act_spec, P('data', 'model', None, None), P(('data', 'model'), None, None), P('data', 'model'), P(('data', 'model'), None), P('data'), P('data'))
    return jax.shard_map(local_layer, mesh=mesh, in_specs=in_specs, out_specs=out_specs, check_vma=False)
```

profile of v0, /device:TPU:21, one launch (start us, length us, event | category | flops | bytes accessed | tf_op | source)
XLA Modules:
  0.0 912.5 jit_solution(8765061334772437856)
XLA Ops:
  7.3 1.5 convert_reduce_fusion.1
  8.8 1.5 fusion.69
  10.2 0.6 copy-done.27
  10.8 0.7 convert_element_type.162
  11.5 2.3 fusion.66
  13.9 0.1 reduce-scatter.5.cloned.1.call-start
  14.0 77.3 %all-gather.5.cloned.1.call-done = bf16[1,4096,1536]{2,1,0:T(8,128)(2,1)} async-done(((bf16[1,256,1536]{2,1,0:T(8,128)(2,1)}), bf16[1,4096,1536]{2,1,0:T(8,128)(2,1)}) %all-gather.5.cloned.1.call-update) | async-done | bytes 12582928 | tf_op jit(solution)/shard_map/all_gather | solution.py:51
  91.3 6.8 fusion.22
  98.2 0.3 convert_bitcast_fusion
  98.6 0.4 copy-done.34
  98.9 26.0 %fusion.84 = (f32[4096]{0:T(1024)S(1)}, f32[4096,4096]{0,1:T(8,128)}) fusion(bf16[1,4096,1,3,96]{1,4,3,2,0:T(8,128)(2,1)S(1)} %convert_bitcast_fusion, s32[4096]{0:T(1024)S(1)} %bitcast.139), kind=kOutput, calls=%fused_computation.118 | convolution fusion | flops 3321884672 | bytes 68730880 | tf_op jit(solution)/shard_map/bqhe,bkhe->bhqk/dot_general | solution.py:24
  124.9 21.3 %fusion.2 = f32[4096]{0:T(1024)S(1)} fusion(f32[4096,4096]{0,1:T(8,128)} %get-tuple-element.19, f32[4096]{0:T(1024)S(1)} %get-tuple-element.18), kind=kLoop, calls=%fused_computation.6 | loop fusion | flops 33550336 | bytes 67141632 | tf_op jit(solution)/shard_map/reduce_sum | solution.py:25
  146.2 0.6 copy-done.18
  146.8 33.2 %fusion.3 = bf16[4096,4096]{0,1:T(8,128)(2,1)} fusion(f32[4096]{0:T(1024)S(1)} %fusion.2, f32[4096,4096]{0,1:T(8,128)} %get-tuple-element.19, f32[4096]{0:T(1024)S(1)} %get-tuple-element.18), kind=kLoop, calls=%fused_computation.8 | loop fusion | flops 50331648 | bytes 100696064 | tf_op jit(solution)/shard_map/convert_element_type | solution.py:26
  180.0 16.2 %fusion.36 = bf16[4096,96]{0,1:T(8,128)(2,1)S(1)} fusion(bf16[4096,4096]{0,1:T(8,128)(2,1)} %fusion.3, bf16[1,4096,1,3,96]{1,4,3,2,0:T(8,128)(2,1)} %copy-done.6), kind=kOutput, calls=%fused_computation.49 | convolution fusion | flops 3221618688 | bytes 35127296 | tf_op jit(solution)/shard_map/bhqk,bkhe->bqhe/dot_general | solution.py:27
  196.2 6.4 fusion.6
  202.7 0.1 all-gather.7.cloned.1.call-start
  202.8 0.5 copy-done.30
  203.3 73.1 %reduce-scatter.5.cloned.1.call-done = bf16[1,256,1536]{2,1,0:T(8,128)(2,1)} async-done(((bf16[1,4096,1536]{2,1,0:T(8,128)(2,1)}), bf16[1,256,1536]{2,1,0:T(8,128)(2,1)}) %reduce-scatter.5.cloned.1.call-update) | async-done | bytes 786448 | tf_op jit(solution)/shard_map/reduce_scatter | solution.py:55
  276.5 1.4 convert_reduce_fusion
  277.9 0.4 fusion.72
  278.3 1.2 fusion.65
  279.5 0.1 all-gather.9.cloned.1.call-start
  279.6 0.6 all-gather.9.cloned.1.call-update
  280.3 72.4 %all-gather.7.cloned.1.call-done = bf16[1,4096,1536]{2,1,0:T(8,128)(2,1)} async-done(((bf16[1,256,1536]{2,1,0:T(8,128)(2,1)}), bf16[1,4096,1536]{2,1,0:T(8,128)(2,1)}) %all-gather.7.cloned.1.call-update) | async-done | bytes 12582928 | tf_op jit(solution)/shard_map/all_gather | solution.py:58
  352.6 11.5 %fusion.18 = f32[4096,384]{1,0:T(8,128)} fusion(bf16[1536,384]{1,0:T(8,128)(2,1)S(1)} %copy-done, bf16[1,4096,1536]{2,1,0:T(8,128)(2,1)} %all-gather.7.cloned.1.call-done), kind=kOutput, calls=%fused_computation.26 | convolution fusion | flops 4831838208 | bytes 20054016 | tf_op jit(solution)/shard_map/bsd,df->bsf/dot_general | solution.py:59
  364.1 60.8 %all-gather.9.cloned.1.call-done = bf16[1,4096,1536]{2,1,0:T(8,128)(2,1)} async-done(((bf16[1,256,1536]{2,1,0:T(8,128)(2,1)}), bf16[1,4096,1536]{2,1,0:T(8,128)(2,1)}) %all-gather.9.cloned.1.call-update) | async-done | bytes 12582928 | tf_op jit(solution)/shard_map/all_gather | solution.py:65
  424.9 14.2 %fusion.30 = bf16[4096,384]{1,0:T(8,128)(2,1)S(1)} fusion(f32[4096,384]{1,0:T(8,128)} %fusion.18, bf16[384,1536]{1,0:T(8,128)(2,1)} %param.16, bf16[1,4096,1536]{2,1,0:T(8,128)(2,1)} %all-gather.9.cloned.1.call-done), kind=kOutput, calls=%fused_computation.40 | convolution fusion | flops 4863295488 | bytes 23199744 | tf_op jit(solution)/shard_map/bsd,fd->bsf/dot_general | solution.py:66
  439.2 1.7 copy-done.35
  440.9 9.6 %fusion.5 = bf16[1,4096,1536]{2,1,0:T(8,128)(2,1)} fusion(bf16[4096,384]{1,0:T(8,128)(2,1)S(1)} %fusion.30, bf16[1536,384]{1,0:T(8,128)(2,1)S(1)} %copy-done), kind=kOutput, calls=%fused_computation.13 | convolution fusion | flops 4838129664 | bytes 16908288 | tf_op jit(solution)/shard_map/bsf,df->bsd/dot_general | solution.py:69
  450.6 0.1 reduce-scatter.7.cloned.1.call-start
  450.7 1.1 copy-done.31
  451.8 15.1 %fusion.4 = bf16[1,4096,1536]{2,1,0:T(8,128)(2,1)} fusion(bf16[384,1536]{1,0:T(8,128)(2,1)S(1)} %copy-done.31, f32[4096,384]{1,0:T(8,128)} %fusion.18), kind=kOutput, calls=%fused_computation.12 | convolution fusion | flops 4852285440 | bytes 20054016 | tf_op jit(solution)/shard_map/bsf,fd->bsd/dot_general | solution.py:62
  467.0 0.1 all-gather.11.cloned.1.call-start
  467.0 57.3 %reduce-scatter.9.cloned.1.call-done = bf16[1,256,1536]{2,1,0:T(8,128)(2,1)} async-done(((bf16[1,4096,1536]{2,1,0:T(8,128)(2,1)}), bf16[1,256,1536]{2,1,0:T(8,128)(2,1)}) %reduce-scatter.9.cloned.1.call-update) | async-done | bytes 786448 | tf_op jit(solution)/shard_map/reduce_scatter | solution.py:71
  524.4 1.6 fusion.73
  526.0 2.5 fusion.67
  528.6 73.8 %reduce-scatter.7.cloned.1.call-done = bf16[1,256,1536]{2,1,0:T(8,128)(2,1)} async-done(((bf16[1,4096,1536]{2,1,0:T(8,128)(2,1)}), bf16[1,256,1536]{2,1,0:T(8,128)(2,1)}) %reduce-scatter.7.cloned.1.call-update) | async-done | bytes 786448 | tf_op jit(solution)/shard_map/reduce_scatter | solution.py:63
  602.4 3.0 add_convert_fusion.1
  605.4 0.1 reduce-scatter.11.cloned.1.call-start
  605.5 73.0 %all-gather.11.cloned.1.call-done = bf16[1,4096,1536]{2,1,0:T(8,128)(2,1)} async-done(((bf16[1,256,1536]{2,1,0:T(8,128)(2,1)}), bf16[1,4096,1536]{2,1,0:T(8,128)(2,1)}) %all-gather.11.cloned.1.call-update) | async-done | bytes 12582928 | tf_op jit(solution)/shard_map/all_gather | solution.py:74
  678.5 8.5 fusion.75
  687.1 15.8 %fusion.35 = bf16[1,4096,1,1,96]{1,4,3,2,0:T(8,128)(2,1)S(1)} fusion(bf16[4096,96]{0,1:T(8,128)(2,1)S(1)} %get-tuple-element.21, bf16[4096,4096]{0,1:T(8,128)(2,1)} %fusion.3), kind=kOutput, calls=%fused_computation.48 | convolution fusion | flops 3221618688 | bytes 35127296 | tf_op jit(solution)/shard_map/bhqk,bqhe->bkhe/dot_general | solution.py:40
  702.9 36.3 %multiply_convert_fusion = bf16[4096,4096]{0,1:T(8,128)(2,1)} fusion(f32[4096]{0:T(1024)S(1)} %get-tuple-element.20, bf16[4096,96]{0,1:T(8,128)(2,1)S(1)} %get-tuple-element.21, f32[4096]{0:T(1024)S(1)} %copy-done.19, f32[4096,4096]{0,1:T(8,128)} %get-tuple-element.19, f32[4096]{0:T(1024)S(1)} %copy-done.17, bf16[1,4096,1,3,96]{1,4,3,2,0:T(8,128)(2,1)S(1)} %copy-done.7), kind=kOutput, calls=%fused_computation | convolution fusion | flops 3321888768 | bytes 102285312 | tf_op jit(solution)/shard_map/bqhe,bkhe->bhqk/dot_general | solution.py:35
  739.2 15.5 %fusion.34 = bf16[1,4096,1,1,96]{1,4,3,2,0:T(8,128)(2,1)S(1)} fusion(bf16[4096,4096]{0,1:T(8,128)(2,1)} %multiply_convert_fusion, bf16[1,4096,1,3,96]{1,4,3,2,0:T(8,128)(2,1)S(1)} %copy-done.7), kind=kOutput, calls=%fused_computation.47 | convolution fusion | flops 3221618688 | bytes 35127296 | tf_op jit(solution)/shard_map/bhqk,bqhe->bkhe/dot_general | solution.py:39
  754.7 13.5 %fusion.37 = bf16[1,4096,1,1,96]{1,4,3,2,0:T(8,128)(2,1)S(1)} fusion(bf16[4096,4096]{0,1:T(8,128)(2,1)} %multiply_convert_fusion, bf16[1,4096,1,3,96]{1,4,3,2,0:T(8,128)(2,1)S(1)} %copy-done.7), kind=kOutput, calls=%fused_computation.50 | convolution fusion | flops 3221618688 | bytes 35127296 | tf_op jit(solution)/shard_map/bhqk,bkhe->bqhe/dot_general | solution.py:38
  768.3 9.6 %fusion.7 = bf16[1,4096,1536]{2,1,0:T(8,128)(2,1)} fusion(bf16[1536,1,3,96]{0,3,2,1:T(8,128)(2,1)S(1)} %copy-done.33, bf16[1,4096,1,1,96]{1,4,3,2,0:T(8,128)(2,1)S(1)} %fusion.35, bf16[1,4096,1,1,96]{1,4,3,2,0:T(8,128)(2,1)S(1)} %fusion.34, bf16[1,4096,1,1,96]{1,4,3,2,0:T(8,128)(2,1)S(1)} %fusion.37), kind=kOutput, calls=%fused_computation.15 | convolution fusion | flops 3632529408 | bytes 15826944 | tf_op jit(solution)/shard_map/bshce,dhce->bsd/dot_general | solution.py:79
  777.9 11.7 %fusion.38 = bf16[1536,384]{1,0:T(8,128)(2,1)} fusion(bf16[4096,384]{1,0:T(8,128)(2,1)} %copy-done.35, bf16[1,4096,1536]{2,1,0:T(8,128)(2,1)} %all-gather.7.cloned.1.call-done), kind=kOutput, calls=%fused_computation.51 | convolution fusion | flops 4832428032 | bytes 16908288 | tf_op jit(solution)/shard_map/bsd,bsf->df/dot_general | solution.py:70
  789.7 12.7 %fusion.41 = bf16[384,1536]{1,0:T(8,128)(2,1)} fusion(bf16[1,4096,1536]{2,1,0:T(8,128)(2,1)} %all-gather.9.cloned.1.call-done, f32[4096,384]{1,0:T(8,128)} %fusion.18), kind=kOutput, calls=%fused_computation.52 | convolution fusion | flops 4846583808 | bytes 20054016 | tf_op jit(solution)/shard_map/bsf,bsd->fd/dot_general | solution.py:68
  802.4 0.6 stack.26
  803.0 0.3 pad_maximum_fusion
  803.4 3.9 fusion.20
  807.2 1.0 convert_bitcast_fusion.1
  808.3 0.5 copy-done.5
  808.8 2.9 fusion.56
  811.7 40.0 %reduce-scatter.11.cloned.1.call-done = bf16[1,256,1536]{2,1,0:T(8,128)(2,1)} async-done(((bf16[1,4096,1536]{2,1,0:T(8,128)(2,1)}), bf16[1,256,1536]{2,1,0:T(8,128)(2,1)}) %reduce-scatter.11.cloned.1.call-update) | async-done | bytes 786448 | tf_op jit(solution)/shard_map/reduce_scatter | solution.py:80
  851.7 1.6 fusion.70
  853.4 0.7 multiply_multiply_fusion.2
  854.1 2.5 fusion.68
  856.6 0.6 pad_maximum_fusion.1
  857.2 44.7 %psum.7 = bf16[2,1536]{1,0:T(2,128)(2,1)S(1)} all-reduce(f32[2,1536]{1,0:T(2,128)} %pad_maximum_fusion.1), channel_id=1, replica_groups=mesh['data'=4,'model'=16] {'model'}, use_global_device_ids=true, to_apply=%region_16.17 | all-reduce | flops 3072 | bytes 18432 | tf_op jit(solution)/shard_map/psum | solution.py:83
  901.9 0.7 negate_multiply_fusion
  902.6 0.6 slice_reduce_fusion
  903.3 2.2 add_convert_fusion
  (96 shorter events, 0.7 us)
Async XLA Ops:
  7.2 345.4 %copy-start = (bf16[1536,384]{1,0:T(8,128)(2,1)S(1)}, bf16[1536,384]{1,0:T(8,128)(2,1)}, u32[]{:S(2)}) copy-start(bf16[1536,384]{1,0:T(8,128)(2,1)} %param.15) | copy-start | bytes 3538948
  7.2 84.1 %copy-start.32 = (bf16[1536,1,3,96]{0,3,2,1:T(8,128)(2,1)S(1)}, bf16[1536,1,3,96]{0,3,2,1:T(8,128)(2,1)}, u32[]{:S(2)}) copy-start(bf16[1536,1,3,96]{0,3,2,1:T(8,128)(2,1)} %param.12) | copy-start | bytes 2654212
  7.2 84.1 %all-gather.5.cloned.1.call-start = ((), (), s32[]{:S(2)}) async-start(), calls=%async_computation.4 | async-start | bytes 13369344 | tf_op jit(solution)/shard_map/all_gather | solution.py:51
  8.7 89.4 %copy-start.20 = (f32[256]{0:T(256)}, f32[256]{0:T(256)S(1)}, u32[]{:S(2)}) copy-start(f32[256]{0:T(256)S(1)} %broadcast_multiply_fusion.1) | copy-start | bytes 3076
  10.2 0.6 copy-start.27
  10.8 87.4 %copy-start.24 = (f32[256]{0:T(256)}, f32[256]{0:T(256)S(1)}, u32[]{:S(2)}) copy-start(f32[256]{0:T(256)S(1)} %fusion.81) | copy-start | bytes 3076
  11.5 86.7 %copy-start.14 = (f32[1536]{0:T(1024)}, f32[1536]{0:T(1024)S(1)}, u32[]{:S(2)}) copy-start(f32[1536]{0:T(1024)S(1)} %convert_element_type.162) | copy-start | bytes 18436
  13.9 262.6 %reduce-scatter.5.cloned.1.call-start = ((), (), s32[]{:S(2)}) async-start(), calls=%async_computation.5 | async-start | bytes 13369344 | tf_op jit(solution)/shard_map/reduce_scatter | solution.py:55
  98.2 0.7 copy-start.34
  98.5 26.4 %copy-start.6 = (bf16[1,4096,1,3,96]{1,4,3,2,0:T(8,128)(2,1)}, bf16[1,4096,1,3,96]{1,4,3,2,0:T(8,128)(2,1)S(1)}, u32[]{:S(2)}) copy-start(bf16[1,4096,1,3,96]{1,4,3,2,0:T(8,128)(2,1)S(1)} %convert_bitcast_fusion) | copy-start | bytes 7077892
  124.9 21.3 %copy-start.16 = (f32[4096]{0:T(1024)}, f32[4096]{0:T(1024)S(1)}, u32[]{:S(2)}) copy-start(f32[4096]{0:T(1024)S(1)} %get-tuple-element.18) | copy-start | bytes 49156
  146.2 0.6 copy-start.18
  180.0 16.2 %copy-start.12 = (bf16[1,96,1536]{2,1,0:T(8,128)(2,1)S(1)}, bf16[1,96,1536]{2,1,0:T(8,128)(2,1)}, u32[]{:S(2)}) copy-start(bf16[1,96,1536]{2,1,0:T(8,128)(2,1)} %param.13) | copy-start | bytes 884740
  196.2 482.3 %copy-start.4 = (bf16[4096,96]{0,1:T(8,128)(2,1)}, bf16[4096,96]{0,1:T(8,128)(2,1)S(1)}, u32[]{:S(2)}) copy-start(bf16[4096,96]{0,1:T(8,128)(2,1)S(1)} %fusion.36) | copy-start | bytes 2359300
  202.6 0.7 copy-start.30
  202.6 73.8 %copy-start.2 = (bf16[1,256,1536]{2,1,0:T(8,128)(2,1)S(1)}, bf16[1,256,1536]{2,1,0:T(8,128)(2,1)}, u32[]{:S(2)}) copy-start(bf16[1,256,1536]{2,1,0:T(8,128)(2,1)} %param.9) | copy-start | bytes 2359300
  202.7 149.9 %all-gather.7.cloned.1.call-start = ((), (), s32[]{:S(2)}) async-start(), calls=%async_computation.6 | async-start | bytes 13369344 | tf_op jit(solution)/shard_map/all_gather | solution.py:58
  278.3 85.8 %copy-start.28 = (f32[256]{0:T(256)}, f32[256]{0:T(256)S(1)}, u32[]{:S(2)}) copy-start(f32[256]{0:T(256)S(1)} %fusion.72) | copy-start | bytes 3076
  279.5 145.4 %all-gather.9.cloned.1.call-start = ((), (), s32[]{:S(2)}) async-start(), calls=%async_computation.8 | async-start | bytes 13369344 | tf_op jit(solution)/shard_map/all_gather | solution.py:65
  280.2 244.2 %reduce-scatter.9.cloned.1.call-start = ((), (), s32[]{:S(2)}) async-start(), calls=%async_computation.9 | async-start | bytes 13369344 | tf_op jit(solution)/shard_map/reduce_scatter | solution.py:71
  439.2 1.7 copy-start.35
  450.5 1.3 copy-start.31
  450.6 151.8 %reduce-scatter.7.cloned.1.call-start = ((), (), s32[]{:S(2)}) async-start(), calls=%async_computation.7 | async-start | bytes 13369344 | tf_op jit(solution)/shard_map/reduce_scatter | solution.py:63
  466.9 59.1 %copy-start.29 = (f32[256]{0:T(256)S(1)}, f32[256]{0:T(256)}, u32[]{:S(2)}) copy-start(f32[256]{0:T(256)} %copy-done.28) | copy-start | bytes 3076
  466.9 135.4 %copy-start.11 = (bf16[1,256,1536]{2,1,0:T(8,128)(2,1)S(1)}, bf16[1,256,1536]{2,1,0:T(8,128)(2,1)}, u32[]{:S(2)}) copy-start(bf16[1,256,1536]{2,1,0:T(8,128)(2,1)} %param.17) | copy-start | bytes 2359300
  467.0 211.5 %all-gather.11.cloned.1.call-start = ((), (), s32[]{:S(2)}) async-start(), calls=%async_computation.10 | async-start | bytes 13369344 | tf_op jit(solution)/shard_map/all_gather | solution.py:74
  524.4 78.0 %copy-start.9 = (bf16[1,256,1536]{2,1,0:T(8,128)(2,1)S(1)}, bf16[1,256,1536]{2,1,0:T(8,128)(2,1)}, u32[]{:S(2)}) copy-start(bf16[1,256,1536]{2,1,0:T(8,128)(2,1)} %reduce-scatter.9.cloned.1.call-done) | copy-start | bytes 2359300
  528.6 149.9 %copy-start.13 = (bf16[1,96,1536]{2,1,0:T(8,128)(2,1)S(1)}, bf16[1,96,1536]{2,1,0:T(8,128)(2,1)}, u32[]{:S(2)}) copy-start(bf16[1,96,1536]{2,1,0:T(8,128)(2,1)} %param.13) | copy-start | bytes 884740
  605.4 246.3 %reduce-scatter.11.cloned.1.call-start = ((), (), s32[]{:S(2)}) async-start(), calls=%async_computation.11 | async-start | bytes 13369344 | tf_op jit(solution)/shard_map/reduce_scatter | solution.py:80
  687.0 15.9 %copy-start.7 = (bf16[1,4096,1,3,96]{1,4,3,2,0:T(8,128)(2,1)S(1)}, bf16[1,4096,1,3,96]{1,4,3,2,0:T(8,128)(2,1)}, u32[]{:S(2)}) copy-start(bf16[1,4096,1,3,96]{1,4,3,2,0:T(8,128)(2,1)} %copy-done.6) | copy-start | bytes 7077892
  687.0 15.9 %copy-start.17 = (f32[4096]{0:T(1024)S(1)}, f32[4096]{0:T(1024)}, u32[]{:S(2)}) copy-start(f32[4096]{0:T(1024)} %copy-done.16) | copy-start | bytes 49156
  687.0 15.9 %copy-start.19 = (f32[4096]{0:T(1024)S(1)}, f32[4096]{0:T(1024)}, u32[]{:S(2)}) copy-start(f32[4096]{0:T(1024)} %copy-done.18) | copy-start | bytes 49156
  754.7 13.5 %copy-start.33 = (bf16[1536,1,3,96]{0,3,2,1:T(8,128)(2,1)S(1)}, bf16[1536,1,3,96]{0,3,2,1:T(8,128)(2,1)}, u32[]{:S(2)}) copy-start(bf16[1536,1,3,96]{0,3,2,1:T(8,128)(2,1)} %param.12) | copy-start | bytes 2654212
  777.9 25.4 %slice-start.3 = ((s8[12582912]{0:T(1024)(128)(4,1)}), s8[4194304]{0:T(1024)(128)(4,1)S(1)}, s32[]{:S(2)}) async-start(s8[12582912]{0:T(1024)(128)(4,1)} %bitcast.136), calls=%async_computation.15 | async-start | bytes 8388608
  789.7 12.8 %copy-start.22 = (f32[1536]{0:T(1024)S(1)}, f32[1536]{0:T(1024)}, u32[]{:S(2)}) copy-start(f32[1536]{0:T(1024)} %get-tuple-element.10) | copy-start | bytes 18436
  789.7 13.6 %slice-start.4 = ((s8[12582912]{0:T(1024)(128)(4,1)}), s8[4194304]{0:T(1024)(128)(4,1)S(1)}, s32[]{:S(2)}) async-start(s8[12582912]{0:T(1024)(128)(4,1)} %bitcast.136), calls=%async_computation.16 | async-start | bytes 8388608
  789.7 13.6 %slice-start.5 = ((s8[12582912]{0:T(1024)(128)(4,1)}), s8[4194304]{0:T(1024)(128)(4,1)S(1)}, s32[]{:S(2)}) async-start(s8[12582912]{0:T(1024)(128)(4,1)} %bitcast.136), calls=%async_computation.17 | async-start | bytes 8388608
  803.0 5.2 slice-start
  803.3 4.9 slice-start.1
  803.4 4.9 slice-start.2
  807.2 1.6 copy-start.5
  808.8 42.9 %copy-start.3 = (bf16[1,256,1536]{2,1,0:T(8,128)(2,1)S(1)}, bf16[1,256,1536]{2,1,0:T(8,128)(2,1)}, u32[]{:S(2)}) copy-start(bf16[1,256,1536]{2,1,0:T(8,128)(2,1)} %param.9) | copy-start | bytes 2359300
  808.8 42.9 %copy-start.15 = (f32[1536]{0:T(1024)S(1)}, f32[1536]{0:T(1024)}, u32[]{:S(2)}) copy-start(f32[1536]{0:T(1024)} %copy-done.14) | copy-start | bytes 18436
  808.8 42.9 %copy-start.21 = (f32[256]{0:T(256)S(1)}, f32[256]{0:T(256)}, u32[]{:S(2)}) copy-start(f32[256]{0:T(256)} %copy-done.20) | copy-start | bytes 3076
  808.8 45.3 %copy-start.25 = (f32[256]{0:T(256)S(1)}, f32[256]{0:T(256)}, u32[]{:S(2)}) copy-start(f32[256]{0:T(256)} %copy-done.24) | copy-start | bytes 3076
  808.8 96.7 %copy-start.1 = (bf16[1536,384]{1,0:T(8,128)(2,1)S(1)}, bf16[1536,384]{1,0:T(8,128)(2,1)}, u32[]{:S(2)}) copy-start(bf16[1536,384]{1,0:T(8,128)(2,1)} %param.15) | copy-start | bytes 3538948
  811.7 91.6 %copy-start.10 = (bf16[1,256,1536]{2,1,0:T(8,128)(2,1)S(1)}, bf16[1,256,1536]{2,1,0:T(8,128)(2,1)}, u32[]{:S(2)}) copy-start(bf16[1,256,1536]{2,1,0:T(8,128)(2,1)} %get-tuple-element.16) | copy-start | bytes 2359300
  851.7 4.9 copy-start.23
  851.7 51.6 %copy-start.8 = (bf16[1,256,1536]{2,1,0:T(8,128)(2,1)S(1)}, bf16[1,256,1536]{2,1,0:T(8,128)(2,1)}, u32[]{:S(2)}) copy-start(bf16[1,256,1536]{2,1,0:T(8,128)(2,1)} %reduce-scatter.11.cloned.1.call-done) | copy-start | bytes 2359300
  854.1 2.5 copy-start.26
Sparse Core Ops, SparseCore 0:
  14.0 77.2 all-gather.4
  202.8 73.6 reduce-scatter.4
  279.7 72.9 all-gather.6
  354.1 70.7 all-gather.8
  450.7 73.6 reduce-scatter.8
  526.6 75.7 reduce-scatter.6
  605.6 72.8 all-gather.10
  778.0 73.6 reduce-scatter.10
where the time goes:
time: 922 us; the launch traced here: 913 us
  waiting for transfers between devices  529 us (57%)
  matrix products  236 us (26%)
  other arithmetic  80.5 us (9%)
  blocking collectives  44.7 us (5%)
  between operations  14.9 us (2%)
    all_gather x1, waiting for transfers between devices, local_layer(): lax.all_gather(ln1_out.astype(jnp.bfloat16), 'model', axis=1, tiled=True)  77.3 us
    reduce_scatter x1, waiting for transfers between devices, local_layer(): lax.psum_scatter(mlp_part, 'model', scatter_dimension=1, tiled=True)  73.8 us
    reduce_scatter x1, waiting for transfers between devices, local_layer(): lax.psum_scatter(attn_part, 'model', scatter_dimension=1, tiled=True)  73.1 us
    all_gather x1, waiting for transfers between devices, local_layer(): d_mid_full = lax.all_gather(d_mid, 'model', axis=1, tiled=True)  73 us
    all_gather x1, waiting for transfers between devices, local_layer(): lax.all_gather(ln2_out.astype(jnp.bfloat16), 'model', axis=1, tiled=True)  72.4 us
    all_gather x1, waiting for transfers between devices, local_layer(): grad_full = lax.all_gather(grad_out, 'model', axis=1, tiled=True)  60.8 us
    reduce_scatter x1, waiting for transfers between devices, local_layer(): lax.psum_scatter(d_mlp_part, 'model', scatter_dimension=1, tiled=True)  57.3 us
    psum x1, blocking collectives, local_layer(): gain_sums = lax.psum(jnp.stack([d_gain_attn, d_gain_mlp]), 'model')  44.7 us
  transfers between devices with their start and end apart: 8, of which 8 were waited for; matrix products, arithmetic and copies ran while one was open for 7% of the time, Pallas kernels for 0%

commit v1 on v0

v1 whole, which is shorter than its diff:
```python
import functools

import jax
import jax.numpy as jnp
from jax import lax
from jax.experimental import pallas as pl
from jax.experimental.pallas import tpu as pltpu
from jax.sharding import PartitionSpec as P

LN_EPS = 1e-5


NEG = -1e30
LOG2E = 1.4426950408889634


def visible_from(pos, cuts):
    first = jnp.zeros_like(pos)
    for n in range(3):
        first = jnp.where(pos >= cuts[n], jnp.maximum(first, cuts[n]), first)
    return first


def attn_fwd_body(dim, blk, cuts_ref, qkv_ref, out_ref, lse_ref, k_nat, m_ref, l_ref, acc):
    seq_len = qkv_ref.shape[1]
    mul = dim ** -0.5 * LOG2E
    cuts = [cuts_ref[n] for n in range(3)]

    def span(n):
        return pl.ds(pl.multiple_of(n * blk, blk), blk)

    @pl.loop(0, seq_len // blk)
    def _(n):
        k_nat[span(n), :] = qkv_ref[dim:2 * dim, span(n)].T

    @pl.loop(0, seq_len // blk)
    def _(i):
        q_t = qkv_ref[0:dim, span(i)]
        q_pos = i * blk + lax.broadcasted_iota(jnp.int32, (1, blk), 1)
        q_first = visible_from(q_pos, cuts)

        def block(j, kind):
            scores = jnp.dot(k_nat[span(j), :], q_t, preferred_element_type=jnp.float32) * mul
            if kind:
                k_pos = j * blk + lax.broadcasted_iota(jnp.int32, (blk, blk), 0)
                seen = k_pos >= q_first
                if kind == 2:
                    seen = seen & (k_pos <= q_pos)
                scores = jnp.where(seen, scores, NEG)
            top = jnp.max(scores, axis=0, keepdims=True)
            v_t = qkv_ref[2 * dim:3 * dim, span(j)]
            if kind == 2:
                prob = jnp.exp2(scores - top)
                m_ref[...] = top
                l_ref[...] = jnp.sum(prob, axis=0, keepdims=True)
                acc[...] = jnp.dot(v_t, prob.astype(jnp.bfloat16), preferred_element_type=jnp.float32)
            else:
                old = m_ref[...]
                top = jnp.maximum(old, top)
                prob = jnp.exp2(scores - top)
                fade = jnp.exp2(old - top)
                m_ref[...] = top
                l_ref[...] = l_ref[...] * fade + jnp.sum(prob, axis=0, keepdims=True)
                acc[...] = acc[...] * fade + jnp.dot(v_t, prob.astype(jnp.bfloat16), preferred_element_type=jnp.float32)

        block(i, 2)
        low = visible_from(i * blk, cuts) // blk
        whole = visible_from(i * blk + blk - 1, cuts)

        @pl.loop(low, i)
        def _(j):
            @pl.when(whole <= j * blk)
            def _():
                block(j, 0)

            @pl.when(whole > j * blk)
            def _():
                block(j, 1)

        total = l_ref[...]
        out_ref[:, span(i)] = (acc[...] / total).astype(jnp.bfloat16)
        lse_ref[:, span(i)] = m_ref[...] + jnp.log2(total)


def attn_fwd(qkv_t, cuts, dim, blk=512):
    seq_len = qkv_t.shape[1]
    return pl.pallas_call(
        functools.partial(attn_fwd_body, dim, blk),
        name="attn_fwd",
        out_shape=(jax.ShapeDtypeStruct((dim, seq_len), jnp.bfloat16), jax.ShapeDtypeStruct((1, seq_len), jnp.float32)),
        in_specs=[pl.BlockSpec(memory_space=pltpu.SMEM), pl.BlockSpec(memory_space=pltpu.VMEM)],
        out_specs=(pl.BlockSpec(memory_space=pltpu.VMEM),) * 2,
        scratch_shapes=[
            pltpu.VMEM((seq_len, dim), jnp.bfloat16),
            pltpu.VMEM((1, blk), jnp.float32),
            pltpu.VMEM((1, blk), jnp.float32),
            pltpu.VMEM((dim, blk), jnp.float32),
        ],
        cost_estimate=pl.CostEstimate(flops=2 * 2 * seq_len * seq_len * dim // 2, bytes_accessed=8 * dim * seq_len, transcendentals=seq_len * seq_len // 2),
        compiler_params=pltpu.CompilerParams(vmem_limit_bytes=40 << 20),
    )(cuts, qkv_t)


def attn_bwd_body(dim, blk, cuts_ref, qkv_ref, o_ref, do_ref, lse_ref, d_ref, k_nat, v_nat, delta, dq_acc, dk_acc, dv_acc):
    seq_len = qkv_ref.shape[1]
    scale = dim ** -0.5
    mul = scale * LOG2E
    count = seq_len // blk
    cuts = [cuts_ref[n] for n in range(3)]
    last_dims = (((1,), (1,)), ((), ()))

    def span(n):
        return pl.ds(pl.multiple_of(n * blk, blk), blk)

    @pl.loop(0, count)
    def _(n):
        k_nat[span(n), :] = qkv_ref[dim:2 * dim, span(n)].T
        v_nat[span(n), :] = qkv_ref[2 * dim:3 * dim, span(n)].T
        delta[:, span(n)] = jnp.sum(do_ref[:, span(n)].astype(jnp.float32) * o_ref[:, span(n)].astype(jnp.float32), axis=0, keepdims=True)
        dq_acc[:, span(n)] = jnp.zeros((dim, blk), jnp.float32)

    @pl.loop(0, count)
    def _(j):
        k_t = qkv_ref[dim:2 * dim, span(j)]

        def block(i, kind):
            q_t = qkv_ref[0:dim, span(i)]
            do_t = do_ref[:, span(i)]
            scores = jnp.dot(k_nat[span(j), :], q_t, preferred_element_type=jnp.float32) * mul
            prob = jnp.exp2(scores - lse_ref[:, span(i)])
            if kind:
                q_pos = i * blk + lax.broadcasted_iota(jnp.int32, (1, blk), 1)
                k_pos = j * blk + lax.broadcasted_iota(jnp.int32, (blk, blk), 0)
                seen = k_pos >= visible_from(q_pos, cuts)
                if kind == 2:
                    seen = seen & (k_pos <= q_pos)
                prob = jnp.where(seen, prob, 0.0)
            d_prob = jnp.dot(v_nat[span(j), :], do_t, preferred_element_type=jnp.float32)
            d_scores = (prob * (d_prob - delta[:, span(i)]) * scale).astype(jnp.bfloat16)
            d_v = lax.dot_general(prob.astype(jnp.bfloat16), do_t, last_dims, preferred_element_type=jnp.float32)
            d_k = lax.dot_general(d_scores, q_t, last_dims, preferred_element_type=jnp.float32)
            if kind == 2:
                dv_acc[...] = d_v
                dk_acc[...] = d_k
            else:
                dv_acc[...] += d_v
                dk_acc[...] += d_k
            dq_acc[:, span(i)] += jnp.dot(k_t, d_scores, preferred_element_type=jnp.float32)

        block(j, 2)

        @pl.loop(j + 1, count)
        def _(i):
            near = visible_from(i * blk, cuts)
            far = visible_from(i * blk + blk - 1, cuts)

            @pl.when(far <= j * blk)
            def _():
                block(i, 0)

            @pl.when((far > j * blk) & (near < (j + 1) * blk))
            def _():
                block(i, 1)

        d_ref[dim:2 * dim, span(j)] = dk_acc[...].T.astype(jnp.bfloat16)
        d_ref[2 * dim:3 * dim, span(j)] = dv_acc[...].T.astype(jnp.bfloat16)

    @pl.loop(0, count)
    def _(n):
        d_ref[0:dim, span(n)] = dq_acc[:, span(n)].astype(jnp.bfloat16)


def attn_bwd(qkv_t, o_t, do_t, lse, cuts, dim, blk=512):
    seq_len = qkv_t.shape[1]
    return pl.pallas_call(
        functools.partial(attn_bwd_body, dim, blk),
        name="attn_bwd",
        out_shape=jax.ShapeDtypeStruct((3 * dim, seq_len), jnp.bfloat16),
        in_specs=[pl.BlockSpec(memory_space=pltpu.SMEM)] + [pl.BlockSpec(memory_space=pltpu.VMEM)] * 4,
        out_specs=pl.BlockSpec(memory_space=pltpu.VMEM),
        scratch_shapes=[
            pltpu.VMEM((seq_len, dim), jnp.bfloat16),
            pltpu.VMEM((seq_len, dim), jnp.bfloat16),
            pltpu.VMEM((1, seq_len), jnp.float32),
            pltpu.VMEM((dim, seq_len), jnp.float32),
            pltpu.VMEM((blk, dim), jnp.float32),
            pltpu.VMEM((blk, dim), jnp.float32),
        ],
        cost_estimate=pl.CostEstimate(flops=2 * 5 * seq_len * seq_len * dim // 2, bytes_accessed=16 * dim * seq_len, transcendentals=seq_len * seq_len // 2),
        compiler_params=pltpu.CompilerParams(vmem_limit_bytes=40 << 20),
    )(cuts, qkv_t, o_t, do_t, lse)


def layer_norm(x_f32, gain_f32):
    mean_val = jnp.mean(x_f32, axis=-1, keepdims=True)
    centered = x_f32 - mean_val
    variance = jnp.mean(centered * centered, axis=-1, keepdims=True)
    return centered * lax.rsqrt(variance + LN_EPS) * gain_f32


def gelu_tanh(pre_act):
    return jax.nn.gelu(pre_act, approximate=True)


def dot(a, b, dims):
    return lax.dot_general(a, b, ((dims[0:1], dims[1:2]), ((), ())), preferred_element_type=jnp.float32)


def local_layer(hidden_in, seg_ids, gain_attn, w_qkv, w_out, gain_mlp, w_up, w_down, grad_out):
    dim = w_out.shape[1]
    hidden = w_out.shape[2]
    x = hidden_in[0]
    dy = grad_out[0]
    cuts = jnp.sum(seg_ids[0][None, :] < jnp.arange(1, 4, dtype=jnp.int32)[:, None], axis=1, dtype=jnp.int32)
    w_qkv_t = jnp.transpose(w_qkv, (1, 2, 3, 0)).reshape(3 * dim, hidden)
    w_o = w_out[0]
    x_f32 = x.astype(jnp.float32)
    ln1_out, ln1_vjp = jax.vjp(layer_norm, x_f32, gain_attn.astype(jnp.float32))
    attn_in = lax.all_gather(ln1_out.astype(jnp.bfloat16), 'model', axis=0, tiled=True)
    qkv_t = dot(w_qkv_t, attn_in, (1, 1)).astype(jnp.bfloat16)
    o_t, lse = attn_fwd(qkv_t, cuts, dim)
    attn_part = dot(o_t, w_o, (0, 0)).astype(jnp.bfloat16)
    attn_sum = lax.psum_scatter(attn_part, 'model', scatter_dimension=0, tiled=True)
    mid_loc = (x_f32 + attn_sum.astype(jnp.float32)).astype(jnp.bfloat16)
    ln2_out, ln2_vjp = jax.vjp(layer_norm, mid_loc.astype(jnp.float32), gain_mlp.astype(jnp.float32))
    mlp_in = lax.all_gather(ln2_out.astype(jnp.bfloat16), 'model', axis=0, tiled=True)
    pre_act = dot(mlp_in, w_up, (1, 0))
    act_f32, gelu_vjp = jax.vjp(gelu_tanh, pre_act)
    act_lo = act_f32.astype(jnp.bfloat16)
    mlp_part = dot(act_lo, w_down, (1, 0)).astype(jnp.bfloat16)
    mlp_sum = lax.psum_scatter(mlp_part, 'model', scatter_dimension=0, tiled=True)
    hidden_out = (mid_loc.astype(jnp.float32) + mlp_sum.astype(jnp.float32)).astype(jnp.bfloat16)
    grad_full = lax.all_gather(dy, 'model', axis=0, tiled=True)
    d_act = dot(grad_full, w_down, (1, 1))
    d_pre = gelu_vjp(d_act)[0].astype(jnp.bfloat16)
    g_down = dot(act_lo, grad_full, (0, 0)).astype(jnp.bfloat16)
    d_mlp_part = dot(d_pre, w_up, (1, 1)).astype(jnp.bfloat16)
    g_up = dot(mlp_in, d_pre, (0, 0)).astype(jnp.bfloat16)
    d_mlp_in = lax.psum_scatter(d_mlp_part, 'model', scatter_dimension=0, tiled=True)
    d_mid_ln, d_gain_mlp = ln2_vjp(d_mlp_in.astype(jnp.float32))
    d_mid = (dy.astype(jnp.float32) + d_mid_ln).astype(jnp.bfloat16)
    d_mid_full = lax.all_gather(d_mid, 'model', axis=0, tiled=True)
    do_t = dot(w_o, d_mid_full, (1, 1)).astype(jnp.bfloat16)
    g_out = dot(o_t, d_mid_full, (1, 0)).astype(jnp.bfloat16)
    d_qkv_t = attn_bwd(qkv_t, o_t, do_t, lse, cuts, dim)
    g_qkv_t = dot(d_qkv_t, attn_in, (1, 0)).astype(jnp.bfloat16)
    g_qkv = jnp.transpose(g_qkv_t.reshape(1, 3, dim, hidden), (3, 0, 1, 2))
    d_attn_part = dot(d_qkv_t, w_qkv_t, (0, 0)).astype(jnp.bfloat16)
    d_attn_in = lax.psum_scatter(d_attn_part, 'model', scatter_dimension=0, tiled=True)
    d_x_ln, d_gain_attn = ln1_vjp(d_attn_in.astype(jnp.float32))
    grad_in = (d_mid.astype(jnp.float32) + d_x_ln).astype(jnp.bfloat16)
    gain_sums = lax.psum(jnp.stack([d_gain_attn, d_gain_mlp]), 'model')
    return (hidden_out[None], grad_in[None], g_qkv, g_out[None], g_up, g_down, gain_sums[0].astype(jnp.bfloat16), gain_sums[1].astype(jnp.bfloat16))


def solution(mesh):
    act_spec = P('data', 'model', None)
    in_specs = (act_spec, P('data', None), P(), P(None, 'model', None, None), P('model', None, None), P(), P(None, 'model'), P('model', None), act_spec)
    out_specs = (act_spec, act_spec, P('data', 'model', None, None), P(('data', 'model'), None, None), P('data', 'model'), P(('data', 'model'), None), P('data'), P('data'))
    return jax.shard_map(local_layer, mesh=mesh, in_specs=in_specs, out_specs=out_specs, check_vma=False)
```

time: 922 us -> 792 us (0.86)
  matrix products: 236 us -> 122 us
  other arithmetic: 80.5 us -> 22.6 us
  Pallas kernels: 0 us -> 42.2 us
    dot_general x16 -> x12, matrix products: 226 us -> 122 us  [dot(): lax.dot_general(a, b, ((dims[0:1], dims[1:2]), ((), ())), preferred_eleme...]
    pallas_call x0 -> x2, Pallas kernels: none -> 42.2 us  [the longest x1 24.3 us: attn_bwd(): pl.pallas_call(functools.partial(attn_bwd_body, dim, blk), name='attn_bwd...]
    convert_element_type x5 -> x1, other arithmetic: 39.7 us -> 3.5 us  [local_layer(): d_mid = (dy.astype(jnp.float32) + d_mid_ln).astype(jnp.bfloat16)]
    reduce_sum x1, other arithmetic: 21.3 us -> 0.21 us  [local_layer(): jnp.sum(seg_ids[0][None, :] < jnp.arange(1, 4, dtype=jnp.int32)[:, None],...]
    unnamed x2 -> x0, matrix products: 10.7 us -> none
  transfers between devices with their start and end apart: 8 -> 8, of which waited for: 8 -> 8; matrix products, arithmetic and copies ran while one was open for 7% -> 8% of each run, Pallas kernels for 0% -> 0%
where the time goes in v1:
time: 792 us; the launch traced here: 780 us
  waiting for transfers between devices  525 us (66%)
  matrix products  122 us (15%)
  blocking collectives  44.8 us (6%)
  Pallas kernels  42.2 us (5%)
  other arithmetic  22.6 us (3%)
  between operations  14.6 us (2%)
    dot_general x12, matrix products, dot(): lax.dot_general(a, b, ((dims[0:1], dims[1:2]), ((), ())), preferred_eleme...  122 us
    all_gather x1, waiting for transfers between devices, local_layer(): lax.all_gather(ln1_out.astype(jnp.bfloat16), 'model', axis=0, tiled=True)  77.1 us
    reduce_scatter x1, waiting for transfers between devices, local_layer(): lax.psum_scatter(mlp_part, 'model', scatter_dimension=0, tiled=True)  74.5 us
    all_gather x1, waiting for transfers between devices, local_layer(): d_mid_full = lax.all_gather(d_mid, 'model', axis=0, tiled=True)  72.6 us
    all_gather x1, waiting for transfers between devices, local_layer(): lax.all_gather(ln2_out.astype(jnp.bfloat16), 'model', axis=0, tiled=True)  72.2 us
    reduce_scatter x1, waiting for transfers between devices, local_layer(): lax.psum_scatter(attn_part, 'model', scatter_dimension=0, tiled=True)  71.6 us
    all_gather x1, waiting for transfers between devices, local_layer(): grad_full = lax.all_gather(dy, 'model', axis=0, tiled=True)  61 us
    reduce_scatter x1, waiting for transfers between devices, local_layer(): lax.psum_scatter(d_mlp_part, 'model', scatter_dimension=0, tiled=True)  57.9 us
  transfers between devices with their start and end apart: 8, of which 8 were waited for; matrix products, arithmetic and copies ran while one was open for 8% of the time, Pallas kernels for 0%

profile of v1, /device:TPU:21, one launch (start us, length us, event | category | flops | bytes accessed | tf_op | source)
XLA Modules:
  0.0 779.8 jit_solution(15695288528401243147)
XLA Ops:
  7.2 0.0 copy-start
  7.2 0.0 copy-start.14
  7.2 0.1 all-gather.6.cloned.1.call-start
  7.3 1.4 convert_reduce_fusion.1
  8.7 1.5 fusion.35
  10.2 0.7 convert_element_type.106
  10.9 2.3 fusion.34
  13.3 0.1 all-gather.6.cloned.1.call-update
  13.3 0.1 reduce-scatter.5.cloned.1.call-start
  13.4 0.2 convert_reduce_fusion.2.cuts_ref
  13.6 77.1 %all-gather.6.cloned.1.call-done = bf16[4096,1536]{1,0:T(8,128)(2,1)} async-done(((bf16[256,1536]{1,0:T(8,128)(2,1)}), bf16[4096,1536]{1,0:T(8,128)(2,1)}) %all-gather.6.cloned.1.call-update) | async-done | bytes 12582928 | tf_op jit(solution)/shard_map/all_gather | solution.py:219
  90.7 13.0 %fusion.11.qkv_ref = bf16[288,4096]{1,0:T(8,128)(2,1)S(1)} fusion(bf16[4096,1536]{1,0:T(8,128)(2,1)} %all-gather.6.cloned.1.call-done, bf16[288,1536]{1,0:T(8,128)(2,1)S(1)} %bitcast.92), kind=kOutput, calls=%fused_computation.19 | convolution fusion | flops 3625058304 | bytes 15826944 | tf_op jit(solution)/shard_map/dot_general | solution.py:206
  103.7 0.0 copy-start.10
  103.8 18.0 %attn_fwd.1 = (bf16[96,4096]{1,0:T(8,128)(2,1)S(1)}, f32[1,4096]{1,0:T(1,128)S(1)}) custom-call(s32[3]{0:T(128)S(1)} %convert_reduce_fusion.2.cuts_ref, bf16[288,4096]{1,0:T(8,128)(2,1)S(1)} %fusion.11.qkv_ref), custom_call_target="tpu_custom_call" | custom-call | flops 3221225472 | bytes 3145728 | tf_op jit(solution)/shard_map/attn_fwd/pallas_call | solution.py:87
  121.7 6.3 convolution_convert_fusion.1
  128.1 0.1 reduce-scatter.5.cloned.1.call-update
  128.1 0.1 all-gather.8.cloned.1.call-start
  128.2 0.5 copy-done.12
  128.8 71.6 %reduce-scatter.5.cloned.1.call-done = bf16[256,1536]{1,0:T(8,128)(2,1)} async-done(((bf16[4096,1536]{1,0:T(8,128)(2,1)}), bf16[256,1536]{1,0:T(8,128)(2,1)}) %reduce-scatter.5.cloned.1.call-update) | async-done | bytes 786448 | tf_op jit(solution)/shard_map/reduce_scatter | solution.py:223
  200.4 1.4 convert_reduce_fusion
  201.8 0.3 fusion.40
  202.2 0.5 copy-done.7
  202.7 1.2 fusion.33
  203.9 0.1 all-gather.8.cloned.1.call-update
  203.9 0.1 all-gather.12.cloned.1.call-start
  204.0 0.6 all-gather.12.cloned.1.call-update
  204.6 0.2 reduce-scatter.9.cloned.1.call-start
  204.8 72.2 %all-gather.8.cloned.1.call-done = bf16[4096,1536]{1,0:T(8,128)(2,1)} async-done(((bf16[256,1536]{1,0:T(8,128)(2,1)}), bf16[4096,1536]{1,0:T(8,128)(2,1)}) %all-gather.8.cloned.1.call-update) | async-done | bytes 12582928 | tf_op jit(solution)/shard_map/all_gather | solution.py:226
  277.0 11.3 %fusion.53 = f32[4096,384]{1,0:T(8,128)} fusion(bf16[4096,1536]{1,0:T(8,128)(2,1)} %all-gather.8.cloned.1.call-done, bf16[1536,384]{1,0:T(8,128)(2,1)S(1)} %copy-done), kind=kOutput, calls=%fused_computation.86 | convolution fusion | flops 4831838208 | bytes 20054016 | tf_op jit(solution)/shard_map/dot_general | solution.py:206
  288.3 61.0 %all-gather.12.cloned.1.call-done = bf16[1,4096,1536]{2,1,0:T(8,128)(2,1)} async-done(((bf16[1,256,1536]{2,1,0:T(8,128)(2,1)}), bf16[1,4096,1536]{2,1,0:T(8,128)(2,1)}) %all-gather.12.cloned.1.call-update) | async-done | bytes 12582928 | tf_op jit(solution)/shard_map/all_gather | solution.py:233
  349.3 14.2 %fusion.10 = bf16[4096,384]{1,0:T(8,128)(2,1)S(1)} fusion(f32[4096,384]{1,0:T(8,128)} %fusion.53, bf16[384,1536]{1,0:T(8,128)(2,1)} %param.16, bf16[1,4096,1536]{2,1,0:T(8,128)(2,1)} %all-gather.12.cloned.1.call-done), kind=kOutput, calls=%fused_computation.16 | convolution fusion | flops 4863295488 | bytes 23199744 | tf_op jit(solution)/shard_map/dot_general | solution.py:206
  363.6 1.7 copy-done.16
  365.3 9.8 %convolution_convert_fusion.2 = bf16[4096,1536]{1,0:T(8,128)(2,1)} fusion(bf16[4096,384]{1,0:T(8,128)(2,1)S(1)} %fusion.10, bf16[1536,384]{1,0:T(8,128)(2,1)S(1)} %copy-done), kind=kOutput, calls=%fused_computation.2 | convolution fusion | flops 4838129664 | bytes 16908288 | tf_op jit(solution)/shard_map/dot_general | solution.py:206
  375.0 0.1 reduce-scatter.9.cloned.1.call-update
  375.1 0.3 reduce-scatter.7.cloned.1.call-start
  375.4 0.9 copy-done.13
  376.3 14.5 %convolution_convert_fusion.3 = bf16[4096,1536]{1,0:T(8,128)(2,1)} fusion(bf16[384,1536]{1,0:T(8,128)(2,1)S(1)} %copy-done.13, f32[4096,384]{1,0:T(8,128)} %fusion.53), kind=kOutput, calls=%fused_computation.3 | convolution fusion | flops 4852285440 | bytes 20054016 | tf_op jit(solution)/shard_map/dot_general | solution.py:206
  390.8 0.1 reduce-scatter.7.cloned.1.call-update
  390.8 0.1 all-gather.10.cloned.1.call-start
  390.9 57.9 %reduce-scatter.9.cloned.1.call-done = bf16[256,1536]{1,0:T(8,128)(2,1)} async-done(((bf16[4096,1536]{1,0:T(8,128)(2,1)}), bf16[256,1536]{1,0:T(8,128)(2,1)}) %reduce-scatter.9.cloned.1.call-update) | async-done | bytes 786448 | tf_op jit(solution)/shard_map/reduce_scatter | solution.py:239
  448.9 1.6 fusion.41
  450.4 2.0 fusion.38
  452.4 74.5 %reduce-scatter.7.cloned.1.call-done = bf16[256,1536]{1,0:T(8,128)(2,1)} async-done(((bf16[4096,1536]{1,0:T(8,128)(2,1)}), bf16[256,1536]{1,0:T(8,128)(2,1)}) %reduce-scatter.7.cloned.1.call-update) | async-done | bytes 786448 | tf_op jit(solution)/shard_map/reduce_scatter | solution.py:231
  526.9 3.5 fusion.43
  530.4 0.1 all-gather.10.cloned.1.call-update
  530.4 0.5 reduce-scatter.11.cloned.1.call-start
  530.9 72.6 %all-gather.10.cloned.1.call-done = bf16[4096,1536]{1,0:T(8,128)(2,1)} async-done(((bf16[256,1536]{1,0:T(8,128)(2,1)}), bf16[4096,1536]{1,0:T(8,128)(2,1)}) %all-gather.10.cloned.1.call-update) | async-done | bytes 12582928 | tf_op jit(solution)/shard_map/all_gather | solution.py:242
  603.5 8.5 %fusion.12.do_ref = bf16[96,4096]{1,0:T(8,128)(2,1)S(1)} fusion(bf16[4096,1536]{1,0:T(8,128)(2,1)} %all-gather.10.cloned.1.call-done, bf16[1,96,1536]{2,1,0:T(8,128)(2,1)S(1)} %copy-done.10), kind=kOutput, calls=%fused_computation.21 | convolution fusion | flops 1208352768 | bytes 13664256 | tf_op jit(solution)/shard_map/dot_general | solution.py:206
  612.0 1.7 copy-done.3
  613.6 24.3 %attn_bwd.1 = bf16[288,4096]{1,0:T(8,128)(2,1)S(1)} custom-call(s32[3]{0:T(128)S(1)} %convert_reduce_fusion.2.cuts_ref, bf16[288,4096]{1,0:T(8,128)(2,1)S(1)} %copy-done.3, bf16[96,4096]{1,0:T(8,128)(2,1)S(1)} %get-tuple-element.10.o_ref, bf16[96,4096]{1,0:T(8,128)(2,1)S(1)} %fusion.12.do_ref, f32[1,4096]{1,0:T(1,128)S(1)} %get-tuple-element.11.lse_ref), custom_call_target="tpu_custom_call" | custom-call | flops 8053063680 | bytes 6291456 | tf_op jit(solution)/shard_map/attn_bwd/pallas_call | solution.py:175
  637.9 1.4 copy-done.4
  639.3 9.6 %convolution_convert_fusion = bf16[4096,1536]{1,0:T(8,128)(2,1)} fusion(bf16[288,4096]{1,0:T(8,128)(2,1)S(1)} %attn_bwd.1, bf16[288,1536]{1,0:T(8,128)(2,1)S(1)} %bitcast.93), kind=kOutput, calls=%fused_computation | convolution fusion | flops 3630170112 | bytes 15826944 | tf_op jit(solution)/shard_map/dot_general | solution.py:206
  648.9 0.1 reduce-scatter.11.cloned.1.call-update
  648.9 0.0 slice-start
  648.9 11.7 %convolution_convert_fusion.6 = bf16[1536,384]{1,0:T(8,128)(2,1)} fusion(bf16[4096,1536]{1,0:T(8,128)(2,1)} %all-gather.8.cloned.1.call-done, bf16[4096,384]{1,0:T(8,128)(2,1)} %copy-done.16), kind=kOutput, calls=%fused_computation.23 | convolution fusion | flops 4832428032 | bytes 16908288 | tf_op jit(solution)/shard_map/dot_general | solution.py:206
  660.7 12.7 %fusion.13 = bf16[384,1536]{1,0:T(8,128)(2,1)} fusion(bf16[1,4096,1536]{2,1,0:T(8,128)(2,1)} %all-gather.12.cloned.1.call-done, f32[4096,384]{1,0:T(8,128)} %fusion.53), kind=kOutput, calls=%fused_computation.22 | convolution fusion | flops 4846583808 | bytes 20054016 | tf_op jit(solution)/shard_map/dot_general | solution.py:206
  673.4 2.8 fusion.20
  676.3 7.8 convolution_convert_fusion.7
  684.1 36.9 %reduce-scatter.11.cloned.1.call-done = bf16[256,1536]{1,0:T(8,128)(2,1)} async-done(((bf16[4096,1536]{1,0:T(8,128)(2,1)}), bf16[256,1536]{1,0:T(8,128)(2,1)}) %reduce-scatter.11.cloned.1.call-update) | async-done | bytes 786448 | tf_op jit(solution)/shard_map/reduce_scatter | solution.py:249
  720.9 1.6 fusion.36
  722.6 2.0 fusion.39
  724.7 44.8 %psum.7 = bf16[2,1536]{1,0:T(2,128)(2,1)S(1)} all-reduce(f32[2,1536]{1,0:T(2,128)S(1)} %pad_maximum_fusion), channel_id=1, replica_groups=mesh['data'=4,'model'=16] {'model'}, use_global_device_ids=true, to_apply=%region_15.0 | all-reduce | flops 3072 | bytes 18432 | tf_op jit(solution)/shard_map/psum | solution.py:252
  769.5 0.6 slice_reduce_fusion
  770.1 2.7 fusion.46
  (44 shorter events, 0.2 us)
Async XLA Ops:
  7.2 269.8 %copy-start = (bf16[1536,384]{1,0:T(8,128)(2,1)S(1)}, bf16[1536,384]{1,0:T(8,128)(2,1)}, u32[]{:S(2)}) copy-start(bf16[1536,384]{1,0:T(8,128)(2,1)} %param.15) | copy-start | bytes 3538948
  7.2 6.2 copy-start.11
  7.2 83.5 %copy-start.14 = (bf16[1536,1,3,96]{0,3,2,1:T(8,128)(2,1)S(1)}, bf16[1536,1,3,96]{0,3,2,1:T(8,128)(2,1)}, u32[]{:S(2)}) copy-start(bf16[1536,1,3,96]{0,3,2,1:T(8,128)(2,1)} %param.12) | copy-start | bytes 2654212
  7.2 83.5 %all-gather.6.cloned.1.call-start = ((), (), s32[]{:S(2)}) async-start(), calls=%async_computation.4 | async-start | bytes 13369344 | tf_op jit(solution)/shard_map/all_gather | solution.py:219
  13.3 187.0 %reduce-scatter.5.cloned.1.call-start = ((), (), s32[]{:S(2)}) async-start(), calls=%async_computation.5 | async-start | bytes 13369344 | tf_op jit(solution)/shard_map/reduce_scatter | solution.py:223
  103.7 18.0 %copy-start.2 = (bf16[288,4096]{1,0:T(8,128)(2,1)}, bf16[288,4096]{1,0:T(8,128)(2,1)S(1)}, u32[]{:S(2)}) copy-start(bf16[288,4096]{1,0:T(8,128)(2,1)S(1)} %fusion.11.qkv_ref) | copy-start | bytes 7077892
  103.7 18.0 %copy-start.10 = (bf16[1,96,1536]{2,1,0:T(8,128)(2,1)S(1)}, bf16[1,96,1536]{2,1,0:T(8,128)(2,1)}, u32[]{:S(2)}) copy-start(bf16[1,96,1536]{2,1,0:T(8,128)(2,1)} %param.13) | copy-start | bytes 884740
  128.1 0.7 copy-start.12
  128.1 72.3 %copy-start.6 = (bf16[1,256,1536]{2,1,0:T(8,128)(2,1)S(1)}, bf16[1,256,1536]{2,1,0:T(8,128)(2,1)}, u32[]{:S(2)}) copy-start(bf16[1,256,1536]{2,1,0:T(8,128)(2,1)} %param.9) | copy-start | bytes 2359300
  128.1 148.9 %all-gather.8.cloned.1.call-start = ((), (), s32[]{:S(2)}) async-start(), calls=%async_computation.6 | async-start | bytes 13369344 | tf_op jit(solution)/shard_map/all_gather | solution.py:226
  201.8 0.9 copy-start.7
  203.9 145.3 %all-gather.12.cloned.1.call-start = ((), (), s32[]{:S(2)}) async-start(), calls=%async_computation.11 | async-start | bytes 13369344 | tf_op jit(solution)/shard_map/all_gather | solution.py:233
  204.6 244.3 %reduce-scatter.9.cloned.1.call-start = ((), (), s32[]{:S(2)}) async-start(), calls=%async_computation.8 | async-start | bytes 13369344 | tf_op jit(solution)/shard_map/reduce_scatter | solution.py:239
  363.5 1.7 copy-start.16
  375.0 1.3 copy-start.13
  375.1 151.8 %reduce-scatter.7.cloned.1.call-start = ((), (), s32[]{:S(2)}) async-start(), calls=%async_computation.7 | async-start | bytes 13369344 | tf_op jit(solution)/shard_map/reduce_scatter | solution.py:231
  390.8 58.1 %copy-start.8 = (bf16[256,1536]{1,0:T(8,128)(2,1)S(1)}, bf16[256,1536]{1,0:T(8,128)(2,1)}, u32[]{:S(2)}) copy-start(bf16[256,1536]{1,0:T(8,128)(2,1)} %copy-done.7) | copy-start | bytes 2359300
  390.8 212.6 %all-gather.10.cloned.1.call-start = ((), (), s32[]{:S(2)}) async-start(), calls=%async_computation.9 | async-start | bytes 13369344 | tf_op jit(solution)/shard_map/all_gather | solution.py:242
  530.4 190.5 %reduce-scatter.11.cloned.1.call-start = ((), (), s32[]{:S(2)}) async-start(), calls=%async_computation.10 | async-start | bytes 13369344 | tf_op jit(solution)/shard_map/reduce_scatter | solution.py:249
  611.9 1.7 copy-start.3
  613.6 25.7 %copy-start.15 = (bf16[1536,1,3,96]{0,3,2,1:T(8,128)(2,1)S(1)}, bf16[1536,1,3,96]{0,3,2,1:T(8,128)(2,1)}, u32[]{:S(2)}) copy-start(bf16[1536,1,3,96]{0,3,2,1:T(8,128)(2,1)} %param.12) | copy-start | bytes 2654212
  637.9 1.4 copy-start.4
  648.9 24.5 %slice-start = ((s8[12582912]{0:T(1024)(128)(4,1)}), s8[4194304]{0:T(1024)(128)(4,1)S(1)}, s32[]{:S(2)}) async-start(s8[12582912]{0:T(1024)(128)(4,1)} %bitcast.89), calls=%async_computation.12 | async-start | bytes 8388608
  660.6 12.8 %slice-start.1 = ((s8[12582912]{0:T(1024)(128)(4,1)}), s8[4194304]{0:T(1024)(128)(4,1)S(1)}, s32[]{:S(2)}) async-start(s8[12582912]{0:T(1024)(128)(4,1)} %bitcast.89), calls=%async_computation.13 | async-start | bytes 8388608
  660.7 12.8 %slice-start.2 = ((s8[12582912]{0:T(1024)(128)(4,1)}), s8[4194304]{0:T(1024)(128)(4,1)S(1)}, s32[]{:S(2)}) async-start(s8[12582912]{0:T(1024)(128)(4,1)} %bitcast.89), calls=%async_computation.14 | async-start | bytes 8388608
  673.4 2.9 copy-start.5
  720.9 49.2 %copy-start.9 = (bf16[256,1536]{1,0:T(8,128)(2,1)S(1)}, bf16[256,1536]{1,0:T(8,128)(2,1)}, u32[]{:S(2)}) copy-start(bf16[256,1536]{1,0:T(8,128)(2,1)} %reduce-scatter.11.cloned.1.call-done) | copy-start | bytes 2359300
  722.6 50.2 %copy-start.1 = (bf16[1536,384]{1,0:T(8,128)(2,1)S(1)}, bf16[1536,384]{1,0:T(8,128)(2,1)}, u32[]{:S(2)}) copy-start(bf16[1536,384]{1,0:T(8,128)(2,1)} %param.15) | copy-start | bytes 3538948
Sparse Core Ops, SparseCore 0:
  13.4 77.2 all-gather.5
  128.3 72.0 reduce-scatter.4
  204.1 72.8 all-gather.7
  278.5 70.7 all-gather.11
  375.2 73.6 reduce-scatter.8
  451.1 75.7 reduce-scatter.6
  530.5 72.8 all-gather.9
  649.0 71.8 reduce-scatter.10
